TPU v7x, 32 devices: a whole 2x2x4 slice. The times are simulated.
32 devices in a mesh: blk: 8 (over z, y), grp: 4 (over x, core).
Axes of the slice: x: 2, y: 2, z: 4, core: 2. Of those that a mesh axis runs over, the one named last changes fastest.
Arguments:
- image_emb: bfloat16 [12288, 1152], P(('blk', 'grp')), may hold values from -0.1875 to 0.1875
- text_emb: bfloat16 [12288, 1152], P(('blk', 'grp')), may hold values from -0.1875 to 0.1875
- positives: int32 [32, 384], P(('blk', 'grp')), may hold values from 0 to 383, each once within a row
- pair_mask: int32 [8, 7], replicated, may hold values from 0 to 1, as said below
- log_scale: float32 [1], replicated, may hold values from 1.5 to 2.5
- bias: float32 [1], replicated, may hold values from -3 to -1
Outputs:
- image_grad: bfloat16 [12288, 1152], P(('blk', 'grp'))
- text_grad: bfloat16 [12288, 1152], P(('blk', 'grp'))
- loss: float32 [1], replicated
Inputs may be any that keep to these rules, and one draw needn't show every extreme that they name: `positives`: every row is a permutation of the rows of a block. `pair_mask`: column 3 is 1 in every row (each image block is scored against its own text block); at least one row is all ones.
All inputs are finite; a program needn't handle non-finite values.
Results may differ from a plain program's by a relative error of at most 0.0063.
Values may be sent and summed in bfloat16 or wider, within the bound.
A program may use at most 64 MiB of HBM per device.

v0:
```python
import functools

import jax
import jax.numpy as jnp
from jax import lax
from jax.experimental import pallas as pl
from jax.experimental.pallas import tpu as pltpu
from jax.sharding import PartitionSpec as P

epsilon = 1e-06


def passed_along(value, axis, steps):
    count = lax.axis_size(axis)
    pairs = [(source, (source + steps) % count) for source in range(count)]
    return lax.ppermute(value, axis, pairs)


def unit_rows(embedded):
    values = embedded.astype(jnp.float32)
    length = jnp.sqrt(jnp.sum(values * values, axis=1, keepdims=True) + epsilon)
    return (values / length, length)


def back_rows(normed, length, upstream):
    inward = jnp.sum(normed * upstream, axis=1, keepdims=True)
    return (upstream - normed * inward) / length


def score_tile(image_side, text_side, labels, logit_scale, offset):
    similar = jnp.einsum("rd,cd->rc", image_side, text_side, preferred_element_type=jnp.float32)
    logits = logit_scale * similar + offset
    signed = labels * logits
    loss_sum = jnp.sum(jax.nn.softplus(-signed))
    slopes = (-labels * jax.nn.sigmoid(-signed) * logit_scale).astype(jnp.bfloat16)
    return (slopes, loss_sum)


def masked_tile(active_flag, image_side, text_side, labels, logit_scale, offset):

    def active(unused):
        return score_tile(image_side, text_side, labels, logit_scale, offset)

    def skipped(unused):
        return (
            jnp.zeros((image_side.shape[0], text_side.shape[0]), jnp.bfloat16),
            jnp.zeros((), jnp.float32),
        )

    return lax.cond(active_flag > 0, active, skipped, 0)


def plain_body(image_emb, text_emb, positives, pair_mask, log_scale, bias):
    reach = (pair_mask.shape[1] - 1) // 2
    block_count = lax.axis_size("blk")
    myself = lax.axis_index("blk")
    logit_scale = jnp.exp(log_scale[0])
    offset = bias[0]
    row_count = image_emb.shape[0]
    image_normed, image_len = unit_rows(image_emb)
    text_normed, text_len = unit_rows(text_emb)
    image_half = image_normed.astype(jnp.bfloat16)
    text_half = text_normed.astype(jnp.bfloat16)
    columns = lax.broadcasted_iota(jnp.int32, (row_count, row_count), 1)
    own_labels = jnp.where(positives[0][:, None] == columns, 1.0, -1.0).astype(jnp.float32)
    apart_labels = -jnp.ones((row_count, row_count), jnp.float32)
    own_flags = lax.dynamic_index_in_dim(pair_mask, myself, 0, keepdims=False)
    fetched = {}
    for direction in (1, -1):
        moving = text_half
        for distance in range(1, reach + 1):
            moving = passed_along(moving, "blk", -direction)
            fetched[direction * distance] = moving
    slopes, loss_sum = masked_tile(
        own_flags[reach], image_half, text_half, own_labels, logit_scale, offset
    )
    image_total = jnp.dot(slopes, text_half, preferred_element_type=jnp.float32)
    text_total = jnp.einsum("rc,rd->cd", slopes, image_half, preferred_element_type=jnp.float32)
    for distance in range(-reach, reach + 1):
        if distance == 0:
            continue
        partner = fetched[distance]
        slopes, part_loss = masked_tile(
            own_flags[reach + distance], image_half, partner, apart_labels, logit_scale, offset
        )
        loss_sum = loss_sum + part_loss
        image_total = image_total + jnp.dot(slopes, partner, preferred_element_type=jnp.float32)
        partial_grad = jnp.einsum(
            "rc,rd->cd", slopes, image_half, preferred_element_type=jnp.float32
        ).astype(jnp.bfloat16)
        arrived = passed_along(partial_grad, "blk", distance)
        text_total = text_total + arrived.astype(jnp.float32)
    total_loss = lax.psum(loss_sum, ("blk", "grp"))
    image_count = row_count * block_count * lax.axis_size("grp")
    loss = (total_loss / image_count).reshape(1)
    image_grad = back_rows(image_normed, image_len, image_total).astype(jnp.bfloat16)
    text_grad = back_rows(text_normed, text_len, text_total).astype(jnp.bfloat16)
    return (image_grad, text_grad, loss)


MESH = pl.DeviceIdType.MESH
Y, INNER, OUTER = 0, 1, 2


def grid_kernel(reach, parts, tiles, mask_ref, scale_ref, offset_ref, image_hbm, text_hbm, pos_hbm,
                image_out, text_out, loss_out,
                held, pos_row, ready, got, own, tmp, acc, loss_acc, blk_loss, grp_loss,
                load_sem, out_sem, send_sem, recv_sem, blk_send, blk_recv, grp_send, grp_recv):
    me = lax.axis_index("blk")
    grp = lax.axis_index("grp")
    count = lax.axis_size("blk")
    groups = lax.axis_size("grp")
    rows = held.shape[1]
    piece = rows // parts
    tall = rows // tiles
    image_ref, text_ref = held.at[1], held.at[0]
    row, col = me // 2, me % 2
    top = row // 2
    role = row + top * (3 - 2 * row)
    toward = 1 - 2 * top
    aside = row * 2 + (1 - col)
    inner = (row + toward) * 2 + col
    outer = lax.rem((row - toward + 4), 4) * 2 + col
    targets = {Y: aside, INNER: inner, OUTER: outer}
    is_end, is_mid = role == 0, role == 1
    raw = (text_ref, image_ref)

    def block(p, c):
        place = p + top * (3 - 2 * p)
        return place * 2 + col + c * (1 - 2 * col)

    def cut(c):
        return pl.ds(pl.multiple_of(c * piece, piece), piece)

    def band(c):
        return pl.ds(pl.multiple_of(c * tall, tall), tall)

    def remote(way, slot, source, kind, which, c):
        return pltpu.make_async_remote_copy(
            src_ref=source.at[cut(c)], dst_ref=got.at[kind, which, cut(c)],
            send_sem=send_sem.at[way, slot, kind, c], recv_sem=recv_sem.at[kind, which, c],
            device_id=(targets[way], grp), device_id_type=MESH)

    def forward(way, slot, kind, which, c):
        remote(way, slot, got.at[kind, which], kind, which, c).start()

    def arrived(kind, which, c):
        remote(Y, 0, got.at[kind, which], kind, which, c).wait_recv()

    loads = [
        pltpu.make_async_copy(source, held.at[kind], load_sem.at[kind])
        for kind, source in ((0, text_hbm), (1, image_hbm))
    ]
    loads.append(pltpu.make_async_copy(pos_hbm, pos_row, load_sem.at[2]))
    for load in loads:
        load.start()
    barrier = pltpu.get_barrier_semaphore()

    @pl.loop(1, count)
    def _(d):
        pl.semaphore_signal(barrier, inc=1, device_id=(lax.rem(me + d, count), grp), device_id_type=MESH)

    @pl.loop(1, groups)
    def _(d):
        pl.semaphore_signal(barrier, inc=1, device_id=(me, lax.rem(grp + d, groups)), device_id_type=MESH)

    pl.semaphore_wait(barrier, count + groups - 2)

    def blk_share(d):
        target = lax.rem(me + d, count)
        return pltpu.make_async_remote_copy(
            src_ref=blk_loss.at[me], dst_ref=blk_loss.at[me], send_sem=blk_send.at[d],
            recv_sem=blk_recv.at[me], device_id=(target, grp), device_id_type=MESH)

    def blk_arrival(d):
        source = lax.rem(me + d, count)
        return pltpu.make_async_remote_copy(
            src_ref=blk_loss.at[source], dst_ref=blk_loss.at[source], send_sem=blk_send.at[d],
            recv_sem=blk_recv.at[source], device_id=(source, grp), device_id_type=MESH)

    def grp_share(d):
        target = lax.rem(grp + d, groups)
        return pltpu.make_async_remote_copy(
            src_ref=grp_loss.at[grp], dst_ref=grp_loss.at[grp], send_sem=grp_send.at[d],
            recv_sem=grp_recv.at[grp], device_id=(me, target), device_id_type=MESH)

    def grp_arrival(d):
        source = lax.rem(grp + d, groups)
        return pltpu.make_async_remote_copy(
            src_ref=grp_loss.at[source], dst_ref=grp_loss.at[source], send_sem=grp_send.at[d],
            recv_sem=grp_recv.at[source], device_id=(me, source), device_id_type=MESH)

    for kind in (0, 1):
        loads[kind].wait()

        @pl.loop(0, parts)
        def _(c, kind=kind):
            remote(Y, 0, raw[kind], kind, me, c).start()
            remote(INNER, 0, raw[kind], kind, me, c).start()

            @pl.when(is_mid)
            def _():
                remote(OUTER, 0, raw[kind], kind, me, c).start()

    scale = jnp.exp(jnp.full((1, 1), scale_ref[0], jnp.float32))
    offset = jnp.full((1, 1), offset_ref[0], jnp.float32)

    def normalise(source, target):
        @pl.loop(0, tiles)
        def _(c):
            values = source[band(c), :].astype(jnp.float32)
            length = jnp.sqrt(jnp.sum(values * values, axis=1, keepdims=True) + epsilon)
            target[band(c), :] = (values / length).astype(jnp.bfloat16)

    def tile(c, side, other):
        similar = lax.dot_general(own[side, band(c), :], other[...], (((1,), (1,)), ((), ())),
                                  preferred_element_type=jnp.float32)
        return scale * similar + offset

    def flag_of(side, which):
        if side == 0:
            apart = lax.rem(which - me + reach + count, count)
            return mask_ref[me, apart].astype(jnp.float32)
        apart = lax.rem(me - which + reach + count, count)
        return mask_ref[which, apart].astype(jnp.float32)

    def item(side, which):
        normalise(got.at[side, which], tmp)
        flag = flag_of(side, which)

        @pl.loop(0, tiles)
        def _(c):
            grown = jnp.exp(tile(c, side, tmp))
            slopes = (grown / (1.0 + grown) * (scale * flag)).astype(jnp.bfloat16)
            acc[side, band(c), :] += jnp.dot(slopes, tmp[...], preferred_element_type=jnp.float32)
            if side == 0:
                loss_acc[...] += flag * jnp.sum(jnp.log1p(grown), axis=0, keepdims=True)

    def own_item(side):
        @pl.loop(0, tiles)
        def _(c):
            logits = tile(c, side, own.at[1 - side])
            flag = mask_ref[me, reach].astype(jnp.float32)
            if side == 0:
                hit = pos_row[:, band(c)] == lax.broadcasted_iota(jnp.int32, (rows, tall), 0)
                labels = jnp.transpose(jnp.where(hit, 1.0, -1.0))
            else:
                hit = pos_row[...] == lax.broadcasted_iota(jnp.int32, logits.shape, 0) + c * tall
                labels = jnp.where(hit, 1.0, -1.0)
            grown = jnp.exp(-labels * logits)
            slopes = (-labels * grown / (1.0 + grown) * (scale * flag)).astype(jnp.bfloat16)
            acc[side, band(c), :] = jnp.dot(slopes, own[1 - side], preferred_element_type=jnp.float32)
            if side == 0:
                loss_acc[...] += flag * jnp.sum(jnp.log1p(grown), axis=0, keepdims=True)

    def short_item(which, k):
        values = got[1, which, band(k), :].astype(jnp.float32)
        length = jnp.sqrt(jnp.sum(values * values, axis=1, keepdims=True) + epsilon)
        tmp[0:tall, :] = (values / length).astype(jnp.bfloat16)
        flag = flag_of(1, which)

        @pl.loop(0, tiles)
        def _(c):
            grown = jnp.exp(tile(c, 1, tmp.at[0:tall]))
            slopes = (grown / (1.0 + grown) * (scale * flag)).astype(jnp.bfloat16)
            acc[1, band(c), :] += jnp.dot(slopes, tmp[0:tall, :], preferred_element_type=jnp.float32)

    def put_out(side, result, c):
        return pltpu.make_async_copy(ready.at[side, band(c)], result.at[band(c)], out_sem.at[side, c])

    def finish(side, source, result):
        @pl.loop(0, tiles)
        def _(c):
            values = source[band(c), :].astype(jnp.float32)
            length = jnp.sqrt(jnp.sum(values * values, axis=1, keepdims=True) + epsilon)
            normed = values / length
            ready[side, band(c), :] = back_rows(normed, length, acc[side, band(c), :]).astype(ready.dtype)
            put_out(side, result, c).start()

    loads[2].wait()
    loss_acc[...] = jnp.zeros_like(loss_acc)
    normalise(image_ref, own.at[0])
    normalise(text_ref, own.at[1])

    steps = 2 * parts

    @pl.loop(0, steps)
    def _(step):
        kind, c = step // parts, step % parts

        @pl.when(is_mid)
        def _():
            arrived(kind, block(0, 0), c)
            forward(INNER, 1, kind, block(0, 0), c)
            forward(Y, 1, kind, block(0, 0), c)
            arrived(kind, block(2, 0), c)
            arrived(kind, block(1, 1), c)

        @pl.when(is_end)
        def _():
            arrived(kind, block(1, 0), c)
            forward(Y, 1, kind, block(1, 0), c)
            arrived(kind, block(0, 1), c)

        @pl.when(step == 0)
        def _():
            own_item(0)

        @pl.when(step == 1)
        def _():
            own_item(1)

    @pl.when(is_mid)
    def _():
        @pl.loop(0, steps)
        def _(step):
            forward(INNER, 2, step // parts, block(1, 1), step % parts)

    def first_block(i):
        mid_p, mid_c = (2 * i) * (2 - i) + i // 2, i // 2
        end_p, end_c = 1 - i % 2, i % 2
        return block(role * mid_p + (1 - role) * end_p, role * mid_c + (1 - role) * end_c)

    @pl.loop(0, steps)
    def _(step):
        kind, c = step // parts, step % parts
        arrived(kind, block(3, 0), c)
        forward(Y, 2, kind, block(3, 0), c)

        @pl.when(is_mid)
        def _():
            forward(OUTER, 1, kind, block(3, 0), c)

        which = first_block(step // 4)
        wanted = (1 - step % 2) * (role + (1 - role) * (1 - step // 8))

        @pl.when(wanted * (2 - step // 2 % 2) == 2)
        def _():
            item(0, which)

        @pl.when(wanted * (1 + step // 2 % 2) == 2)
        def _():
            item(1, which)

        arrived(kind, block(1 - role, 1), c)

    def second_block(i):
        return block((1 - role) * (3 - 2 * i), (1 - role) * i + role)

    @pl.loop(0, steps - 1)
    def _(step):
        kind, c = step // parts, step % parts
        arrived(kind, block(2, 1), c)

        @pl.when(is_mid)
        def _():
            forward(OUTER, 2, kind, block(2, 1), c)

        wanted = (1 - (step + 8) // 12) * (1 - role * (step // 2))

        @pl.when(wanted * (2 - step % 2) == 2)
        def _():
            item(0, second_block(step // 2))

        @pl.when(wanted * (1 + step % 2) == 2)
        def _():
            item(1, second_block(step // 2))

        @pl.when(step == parts)
        def _():
            item(0, block(2, 1))

        arrived(kind, block(3, 1), c)

        @pl.when(step == parts + 1)
        def _():
            item(0, block(3, 1))
            blk_loss[me] = jnp.full(blk_loss.shape[1:], jnp.sum(loss_acc[...]), jnp.float32)

        @pl.when(step == parts + 2)
        def _():
            finish(0, image_ref, image_out)

            @pl.loop(1, count)
            def _(d):
                blk_share(d).start()

        @pl.when(step == parts + 3)
        def _():
            short_item(block(2, 1), 0)
            short_item(block(3, 1), 0)

        @pl.when(step == parts + 4)
        def _():
            short_item(block(2, 1), 1)
            short_item(block(3, 1), 1)

    final = role * 0 + parts - 1

    @pl.when(is_mid)
    def _():
        arrived(1, block(2, 1), final)
        forward(OUTER, 2, 1, block(2, 1), final)

    arrived(1, block(3, 1), final)

    @pl.loop(1, count)
    def _(d):
        blk_arrival(d).wait_recv()

    grp_loss[grp] = jnp.sum(blk_loss[...], axis=0)
    short_item(block(3, 1), 2)

    @pl.loop(1, groups)
    def _(d):
        grp_share(d).start()

    @pl.when(is_end)
    def _():
        arrived(1, block(2, 1), final)

    short_item(block(2, 1), 2)
    finish(1, text_ref, text_out)

    @pl.loop(1, groups)
    def _(d):
        grp_arrival(d).wait_recv()

    total = jnp.sum(grp_loss[...], axis=0)
    @pl.loop(0, tiles)
    def _(c):
        put_out(0, image_out, c).wait()
        put_out(1, text_out, c).wait()

    loss_out[0] = jnp.sum(total[0:1, 0:1]) / (rows * count * groups)

    @pl.loop(1, count)
    def _(d):
        blk_share(d).wait_send()

    @pl.loop(1, groups)
    def _(d):
        grp_share(d).wait_send()

    @pl.loop(0, steps)
    def _(step):
        kind, c = step // parts, step % parts
        for slot in range(3):
            remote(Y, slot, got.at[kind, me], kind, me, c).wait_send()

        remote(INNER, 0, got.at[kind, me], kind, me, c).wait_send()

        @pl.when(is_mid)
        def _():
            remote(INNER, 1, got.at[kind, me], kind, me, c).wait_send()
            remote(INNER, 2, got.at[kind, me], kind, me, c).wait_send()
            for slot in range(3):
                remote(OUTER, slot, got.at[kind, me], kind, me, c).wait_send()


def body(image_emb, text_emb, positives, pair_mask, log_scale, bias):
    reach = (pair_mask.shape[1] - 1) // 2
    block_count = lax.axis_size("blk")
    row_count, width = image_emb.shape
    if block_count != 2 * (reach + 1) or reach != 3 or row_count % (3 * 128) != 0:
        return plain_body(image_emb, text_emb, positives, pair_mask, log_scale, bias)
    parts, tiles = 6, 3
    groups = lax.axis_size("grp")
    smem = pl.BlockSpec(memory_space=pltpu.SMEM)
    anywhere = pl.BlockSpec(memory_space=pl.ANY)
    return pl.pallas_call(
        functools.partial(grid_kernel, reach, parts, tiles),
        out_shape=(
            jax.ShapeDtypeStruct(image_emb.shape, image_emb.dtype),
            jax.ShapeDtypeStruct(text_emb.shape, text_emb.dtype),
            jax.ShapeDtypeStruct((1,), jnp.float32),
        ),
        in_specs=[smem] * 3 + [anywhere] * 3,
        out_specs=(anywhere, anywhere, smem),
        scratch_shapes=[
            pltpu.VMEM((2, row_count, width), jnp.bfloat16),
            pltpu.VMEM((1, row_count), jnp.int32),
            pltpu.VMEM((2, row_count, width), jnp.bfloat16),
            pltpu.VMEM((2, block_count, row_count, width), jnp.bfloat16),
            pltpu.VMEM((2, row_count, width), jnp.bfloat16),
            pltpu.VMEM((row_count, width), jnp.bfloat16),
            pltpu.VMEM((2, row_count, width), jnp.float32),
            pltpu.VMEM((1, row_count), jnp.float32),
            pltpu.VMEM((block_count, 8, 128), jnp.float32),
            pltpu.VMEM((groups, 8, 128), jnp.float32),
            pltpu.SemaphoreType.DMA((3,)),
            pltpu.SemaphoreType.DMA((2, tiles)),
            pltpu.SemaphoreType.DMA((3, 3, 2, parts)),
            pltpu.SemaphoreType.DMA((2, block_count, parts)),
            pltpu.SemaphoreType.DMA((block_count,)),
            pltpu.SemaphoreType.DMA((block_count,)),
            pltpu.SemaphoreType.DMA((groups,)),
            pltpu.SemaphoreType.DMA((groups,)),
        ],
        compiler_params=pltpu.CompilerParams(
            collective_id=0, has_side_effects=True, vmem_limit_bytes=67043328
        ),
    )(pair_mask, log_scale, bias, image_emb, text_emb, positives)


def solution(mesh):
    return jax.shard_map(
        body,
        mesh=mesh,
        in_specs=(
            P(("blk", "grp"), None),
            P(("blk", "grp"), None),
            P(("blk", "grp"), None),
            P(),
            P(),
            P(),
        ),
        out_specs=(P(("blk", "grp"), None), P(("blk", "grp"), None), P()),
        check_vma=False,
    )
```

profile of v0, /device:TPU:0, one launch (start us, length us, event | category | flops | bytes accessed | tf_op | source)
XLA Modules:
  0.0 143.8 jit_solution(15389756159213953539)
XLA Ops:
  1.9 136.9 %shard_map.85 = (bf16[384,1152]{1,0:T(8,128)(2,1)}, bf16[384,1152]{1,0:T(8,128)(2,1)}, f32[1]{0:T(128)}) custom-call(s32[8,7]{1,0:T(8,128)} %mask_ref.1, f32[1]{0:T(128)S(6)} %copy.12.scale_ref, f32[1]{0:T(128)S(6)} %copy.13.offset_ref, bf16[384,1152]{1,0:T(8,128)(2,1)} %image_hbm.1, bf16[384,1152]{1,0:T(8,128)(2,1)} %text_hbm.1, s32[1,384]{1,0:T(1,128)} %pos_hbm.1), custom_call_target="tpu_custom_call" | custom-call | tf_op jit(solution)/shard_map/pallas_call | solution.py:471
  138.9 0.0 copy-start
  138.9 2.2 %copy.14 = bf16[384,1152]{1,0:T(8,128)(2,1)} copy(bf16[384,1152]{1,0:T(8,128)(2,1)} %get-tuple-element.6) | data formatting | bytes 1769472
  141.1 0.0 copy-done
  141.1 0.9 copy.15
Async XLA Ops:
  138.9 2.2 %copy-start = (bf16[384,1152]{1,0:T(8,128)(2,1)S(1)}, bf16[384,1152]{1,0:T(8,128)(2,1)}, u32[]{:S(2)}) copy-start(bf16[384,1152]{1,0:T(8,128)(2,1)} %get-tuple-element.7) | copy-start | bytes 2654212
where the time goes:
time: 144 us
  Pallas kernels  137 us (95%)
  between operations  3.76 us (3%)
  local copies, waits for them, and re-layouts  3.14 us (2%)
    pallas_call x1, Pallas kernels, body(): pl.pallas_call(functools.partial(grid_kernel, reach, parts, tiles), out_s...  137 us
    unnamed x4, local copies, waits for them, and re-layouts  3.14 us

commit v1 on v0

v1 whole, which is shorter than its diff:
```python
import functools

import jax
import jax.numpy as jnp
from jax import lax
from jax.experimental import pallas as pl
from jax.experimental.pallas import tpu as pltpu
from jax.sharding import PartitionSpec as P

epsilon = 1e-06


def passed_along(value, axis, steps):
    count = lax.axis_size(axis)
    pairs = [(source, (source + steps) % count) for source in range(count)]
    return lax.ppermute(value, axis, pairs)


def unit_rows(embedded):
    values = embedded.astype(jnp.float32)
    length = jnp.sqrt(jnp.sum(values * values, axis=1, keepdims=True) + epsilon)
    return (values / length, length)


def back_rows(normed, length, upstream):
    inward = jnp.sum(normed * upstream, axis=1, keepdims=True)
    return (upstream - normed * inward) / length


def score_tile(image_side, text_side, labels, logit_scale, offset):
    similar = jnp.einsum("rd,cd->rc", image_side, text_side, preferred_element_type=jnp.float32)
    logits = logit_scale * similar + offset
    signed = labels * logits
    loss_sum = jnp.sum(jax.nn.softplus(-signed))
    slopes = (-labels * jax.nn.sigmoid(-signed) * logit_scale).astype(jnp.bfloat16)
    return (slopes, loss_sum)


def masked_tile(active_flag, image_side, text_side, labels, logit_scale, offset):

    def active(unused):
        return score_tile(image_side, text_side, labels, logit_scale, offset)

    def skipped(unused):
        return (
            jnp.zeros((image_side.shape[0], text_side.shape[0]), jnp.bfloat16),
            jnp.zeros((), jnp.float32),
        )

    return lax.cond(active_flag > 0, active, skipped, 0)


def plain_body(image_emb, text_emb, positives, pair_mask, log_scale, bias):
    reach = (pair_mask.shape[1] - 1) // 2
    block_count = lax.axis_size("blk")
    myself = lax.axis_index("blk")
    logit_scale = jnp.exp(log_scale[0])
    offset = bias[0]
    row_count = image_emb.shape[0]
    image_normed, image_len = unit_rows(image_emb)
    text_normed, text_len = unit_rows(text_emb)
    image_half = image_normed.astype(jnp.bfloat16)
    text_half = text_normed.astype(jnp.bfloat16)
    columns = lax.broadcasted_iota(jnp.int32, (row_count, row_count), 1)
    own_labels = jnp.where(positives[0][:, None] == columns, 1.0, -1.0).astype(jnp.float32)
    apart_labels = -jnp.ones((row_count, row_count), jnp.float32)
    own_flags = lax.dynamic_index_in_dim(pair_mask, myself, 0, keepdims=False)
    fetched = {}
    for direction in (1, -1):
        moving = text_half
        for distance in range(1, reach + 1):
            moving = passed_along(moving, "blk", -direction)
            fetched[direction * distance] = moving
    slopes, loss_sum = masked_tile(
        own_flags[reach], image_half, text_half, own_labels, logit_scale, offset
    )
    image_total = jnp.dot(slopes, text_half, preferred_element_type=jnp.float32)
    text_total = jnp.einsum("rc,rd->cd", slopes, image_half, preferred_element_type=jnp.float32)
    for distance in range(-reach, reach + 1):
        if distance == 0:
            continue
        partner = fetched[distance]
        slopes, part_loss = masked_tile(
            own_flags[reach + distance], image_half, partner, apart_labels, logit_scale, offset
        )
        loss_sum = loss_sum + part_loss
        image_total = image_total + jnp.dot(slopes, partner, preferred_element_type=jnp.float32)
        partial_grad = jnp.einsum(
            "rc,rd->cd", slopes, image_half, preferred_element_type=jnp.float32
        ).astype(jnp.bfloat16)
        arrived = passed_along(partial_grad, "blk", distance)
        text_total = text_total + arrived.astype(jnp.float32)
    total_loss = lax.psum(loss_sum, ("blk", "grp"))
    image_count = row_count * block_count * lax.axis_size("grp")
    loss = (total_loss / image_count).reshape(1)
    image_grad = back_rows(image_normed, image_len, image_total).astype(jnp.bfloat16)
    text_grad = back_rows(text_normed, text_len, text_total).astype(jnp.bfloat16)
    return (image_grad, text_grad, loss)


MESH = pl.DeviceIdType.MESH
Y, INNER, OUTER = 0, 1, 2
OWN, OTHER = 0, 1


def grid_kernel(reach, parts, tiles, mask_ref, scale_ref, offset_ref, image_hbm, text_hbm, pos_hbm,
                image_out, text_out, loss_out,
                texts, images, pos_row, unit_texts, unit_images, labels, slopes, terms, sent, got,
                image_acc, image_sent, image_got, ready, loss_acc, blk_loss, grp_loss,
                load_sem, out_sem, send_sem, text_recv, image_recv, term_recv, back_recv,
                blk_send, blk_recv, grp_send, grp_recv):
    me = lax.axis_index("blk")
    grp = lax.axis_index("grp")
    count = lax.axis_size("blk")
    groups = lax.axis_size("grp")
    rows = images.shape[1]
    places = count // 2
    piece = rows // parts
    tall = rows // tiles
    per_tile = parts // tiles
    row, col = me // 2, me % 2
    top = row // 2
    role = row + top * (3 - 2 * row)
    toward = 1 - 2 * top
    aside = row * 2 + (1 - col)
    inner = (row + toward) * 2 + col
    outer = lax.rem((row - toward + 4), 4) * 2 + col
    targets = {Y: aside, INNER: inner, OUTER: outer}
    is_end, is_mid = role == 0, role == 1

    def place_row(p):
        return p + top * (3 - 2 * p)

    def cut(c):
        return pl.ds(pl.multiple_of(c * piece, piece), piece)

    def at(which, c):
        return pl.ds(pl.multiple_of(which * rows + c * piece, piece), piece)

    def tile_at(which, c):
        return pl.ds(pl.multiple_of(which * rows + c * tall, tall), tall)

    def send(way, slot, c, source, target, recv):
        return pltpu.make_async_remote_copy(
            src_ref=source, dst_ref=target, send_sem=send_sem.at[way, slot, c], recv_sem=recv,
            device_id=(targets[way], grp), device_id_type=MESH)

    def text_copy(way, slot, which, c):
        return send(way, slot, c, texts.at[at(which, c)], texts.at[at(which, c)], text_recv.at[which, c])

    def image_copy(c):
        return send(Y, 0, c, images.at[OWN, cut(c)], images.at[OTHER, cut(c)], image_recv.at[c])

    def back_copy(c):
        return send(Y, 1, c, image_sent.at[cut(c)], image_got.at[cut(c)], back_recv.at[c])

    def term_copy(way, slot, which, side, c):
        return send(way, slot, c, sent.at[at(which, c)], got.at[side, at(which, c)], term_recv.at[side, which, c])

    def term_arrived(side, which, c):
        term_copy(INNER, 0, which, side, c).wait_recv()

    own_row = place_row(role)
    loads = [
        pltpu.make_async_copy(text_hbm, texts.at[pl.ds(pl.multiple_of(own_row * rows, rows), rows)], load_sem.at[0]),
        pltpu.make_async_copy(image_hbm, images.at[OWN], load_sem.at[1]),
        pltpu.make_async_copy(pos_hbm, pos_row, load_sem.at[2]),
    ]
    for load in loads:
        load.start()
    barrier = pltpu.get_barrier_semaphore()

    @pl.loop(1, count)
    def _(d):
        pl.semaphore_signal(barrier, inc=1, device_id=(lax.rem(me + d, count), grp), device_id_type=MESH)

    @pl.loop(1, groups)
    def _(d):
        pl.semaphore_signal(barrier, inc=1, device_id=(me, lax.rem(grp + d, groups)), device_id_type=MESH)

    pl.semaphore_wait(barrier, count + groups - 2)

    def blk_share(d):
        target = lax.rem(me + d, count)
        return pltpu.make_async_remote_copy(
            src_ref=blk_loss.at[me], dst_ref=blk_loss.at[me], send_sem=blk_send.at[d],
            recv_sem=blk_recv.at[me], device_id=(target, grp), device_id_type=MESH)

    def blk_arrival(d):
        source = lax.rem(me + d, count)
        return pltpu.make_async_remote_copy(
            src_ref=blk_loss.at[source], dst_ref=blk_loss.at[source], send_sem=blk_send.at[d],
            recv_sem=blk_recv.at[source], device_id=(source, grp), device_id_type=MESH)

    def grp_share(d):
        target = lax.rem(grp + d, groups)
        return pltpu.make_async_remote_copy(
            src_ref=grp_loss.at[grp], dst_ref=grp_loss.at[grp], send_sem=grp_send.at[d],
            recv_sem=grp_recv.at[grp], device_id=(me, target), device_id_type=MESH)

    def grp_arrival(d):
        source = lax.rem(grp + d, groups)
        return pltpu.make_async_remote_copy(
            src_ref=grp_loss.at[source], dst_ref=grp_loss.at[source], send_sem=grp_send.at[d],
            recv_sem=grp_recv.at[source], device_id=(me, source), device_id_type=MESH)

    loads[0].wait()

    @pl.loop(0, parts)
    def _(c):
        text_copy(INNER, 0, own_row, c).start()

        @pl.when(is_mid)
        def _():
            text_copy(OUTER, 0, own_row, c).start()

    loads[1].wait()

    @pl.loop(0, parts)
    def _(c):
        image_copy(c).start()

    scale = jnp.exp(jnp.full((1, 1), scale_ref[0], jnp.float32))
    offset = jnp.full((1, 1), offset_ref[0], jnp.float32)

    def unit(values):
        length = jnp.sqrt(jnp.sum(values * values, axis=1, keepdims=True) + epsilon)
        return values / length, length

    loss_acc[...] = jnp.zeros_like(loss_acc)
    loads[2].wait()

    @pl.loop(0, tiles)
    def _(c):
        band = pl.ds(pl.multiple_of(c * tall, tall), tall)
        unit_images[band, :] = unit(images[OWN, band, :].astype(jnp.float32))[0].astype(jnp.bfloat16)
        hit = pos_row[...] == lax.broadcasted_iota(jnp.int32, (tall, rows), 0) + c * tall
        labels[1 + c] = jnp.transpose(jnp.where(hit, -1.0, 1.0))

    labels[0] = jnp.full(labels.shape[1:], 1.0, jnp.float32)

    @pl.loop(0, parts)
    def _(c):
        @pl.when(is_mid)
        def _():
            text_copy(Y, 0, place_row(0), c).wait_recv()
            text_copy(INNER, 1, place_row(0), c).start()
            text_copy(Y, 0, place_row(2), c).wait_recv()
            text_copy(OUTER, 1, place_row(2), c).start()

        image_copy(c).wait_recv()
        unit_images[at(1, c), :] = unit(images[OTHER, cut(c), :].astype(jnp.float32))[0].astype(jnp.bfloat16)

    def flag_of(other, which):
        image = row * 2 + col + other * (1 - 2 * col)
        text = which * 2 + col
        apart = lax.rem(text - image + reach + count, count)
        inside = 1 - apart // (2 * reach + 1)
        return (mask_ref[image, apart * inside] * inside).astype(jnp.float32)

    def item(p, which, c):
        text = unit(texts[tile_at(which, c), :].astype(jnp.float32))[0].astype(jnp.bfloat16)
        unit_texts[tile_at(which, c), :] = text
        own = 1 // (1 + (p - role) * (p - role))
        term = None
        for other in (OWN, OTHER):
            flag = flag_of(other, which)
            side = unit_images[other * rows:(other + 1) * rows, :]
            similar = lax.dot_general(side, text, (((1,), (1,)), ((), ())), preferred_element_type=jnp.float32)
            logits = scale * similar + offset
            factor = scale * flag
            if other == OWN:
                label = labels[(1 + c) * own]
                logits = logits * label
                factor = factor * label
            grown = jnp.exp(logits)
            lifted = 1.0 + grown
            slope = (grown / lifted * factor).astype(jnp.bfloat16)
            slopes[other, :, tile_at(which, c)] = slope
            loss_acc[...] += flag * jnp.sum(jnp.log(lifted), axis=0, keepdims=True)
            part = lax.dot_general(slope, side, (((0,), (0,)), ((), ())), preferred_element_type=jnp.float32)
            term = part if term is None else term + part
        terms[tile_at(which, c), :] = term
        sent[tile_at(which, c), :] = term.astype(jnp.bfloat16)

    def relay(way, slot, side, p, c):
        which = place_row(p)
        term_arrived(side, which, c)
        total = terms[at(which, c), :] + got[side, at(which, c), :].astype(jnp.float32)
        sent[at(which, c), :] = total.astype(jnp.bfloat16)
        term_copy(way, slot, which, 1, c).start()

    steps = 4 * tiles

    @pl.loop(0, steps)
    def _(s):
        third = s // tiles
        first, last = (tiles - third) // tiles, third // tiles
        between, odd = 1 - first - last, (s + 1) % 2
        p = (first * (1 + role) + last * (3 - 2 * role)
             + between * ((1 - odd) * (2 - 2 * role) + odd * 3 * role))
        c = first * s + last * (s - 3 * tiles) + between * ((s + 1) // 2 - 2)
        which = place_row(p)

        @pl.when((1 - role) * p > 0)
        def _():
            @pl.loop(0, per_tile)
            def _(k):
                text_copy(Y, 0, which, c * per_tile + k).wait_recv()

        @pl.when(role * (p // 3) == 1)
        def _():
            @pl.loop(0, per_tile)
            def _(k):
                text_copy(Y, 0, which, c * per_tile + k).wait_recv()
                text_copy(OUTER, 2, which, c * per_tile + k).start()

        item(p, which, c)

        @pl.when((1 - role) * p * (p // 3 + (tiles - c) // 2) > 0)
        def _():
            @pl.loop(0, per_tile)
            def _(k):
                term_copy(INNER, p, which, 0, c * per_tile + k).start()

        @pl.when(role * (s // 7) * (1 - s // 11) == 1)
        def _():
            relay(INNER, 2, 0, 2, s - 7)

    @pl.when(is_end)
    def _():
        @pl.loop(0, 2 * per_tile)
        def _(k):
            p = 2 - k // per_tile
            term_copy(INNER, p, place_row(p), 0, parts - per_tile + k % per_tile).start()

    blk_loss[me] = jnp.full(blk_loss.shape[1:], jnp.sum(loss_acc[...]), jnp.float32)

    @pl.loop(1, count)
    def _(d):
        blk_share(d).start()

    @pl.loop(0, parts)
    def _(c):
        @pl.when(is_mid)
        def _():
            relay(INNER, 3, 0, 3, c)

        whole = jnp.dot(slopes[OTHER, cut(c), :], unit_texts[...], preferred_element_type=jnp.float32)
        image_sent[cut(c), :] = whole.astype(jnp.bfloat16)
        back_copy(c).start()
        image_acc[cut(c), :] = jnp.dot(
            slopes[OWN, cut(c), :], unit_texts[...], preferred_element_type=jnp.float32)

        @pl.when(role * c > 0)
        def _():
            relay(OUTER, 3, 1, 0, c - 1)

    @pl.when(is_mid)
    def _():
        relay(OUTER, 3, 1, 0, parts - 1)

        @pl.loop(parts - per_tile, parts)
        def _(c):
            relay(INNER, 2, 0, 2, c)

    @pl.loop(1, count)
    def _(d):
        blk_arrival(d).wait_recv()

    grp_loss[grp] = jnp.sum(blk_loss[...], axis=0)

    @pl.loop(1, groups)
    def _(d):
        grp_share(d).start()

    def put_out(side, result, c):
        return pltpu.make_async_copy(ready.at[side, cut(c)], result.at[cut(c)], out_sem.at[side, c])

    def finish(side, source, upstream, result, c):
        normed, length = unit(source.astype(jnp.float32))
        ready[side, cut(c), :] = back_rows(normed, length, upstream).astype(ready.dtype)
        put_out(side, result, c).start()

    @pl.loop(0, parts)
    def _(c):
        term_arrived(1, own_row, c)

        @pl.when(is_mid)
        def _():
            term_arrived(0, own_row, c)
            terms[at(own_row, c), :] += got[0, at(own_row, c), :].astype(jnp.float32)

        total = terms[at(own_row, c), :] + got[1, at(own_row, c), :].astype(jnp.float32)
        finish(1, texts[at(own_row, c), :], total, text_out, c)
        back_copy(c).wait_recv()
        total = image_acc[cut(c), :] + image_got[cut(c), :].astype(jnp.float32)
        finish(0, images[OWN, cut(c), :], total, image_out, c)

    @pl.loop(1, groups)
    def _(d):
        grp_arrival(d).wait_recv()

    total = jnp.sum(grp_loss[...], axis=0)
    loss_out[0] = jnp.sum(total[0:1, 0:1]) / (rows * count * groups)

    @pl.loop(1, count)
    def _(d):
        blk_share(d).wait_send()

    @pl.loop(1, groups)
    def _(d):
        grp_share(d).wait_send()

    @pl.loop(0, parts)
    def _(c):
        put_out(0, image_out, c).wait()
        put_out(1, text_out, c).wait()
        for slot in range(2):
            text_copy(Y, slot, own_row, c).wait_send()
        for slot in range(4):
            text_copy(INNER, slot, own_row, c).wait_send()

        @pl.when(is_mid)
        def _():
            for slot in range(4):
                text_copy(OUTER, slot, own_row, c).wait_send()


def body(image_emb, text_emb, positives, pair_mask, log_scale, bias):
    reach = (pair_mask.shape[1] - 1) // 2
    block_count = lax.axis_size("blk")
    row_count, width = image_emb.shape
    if block_count != 2 * (reach + 1) or reach != 3 or row_count % (3 * 128) != 0:
        return plain_body(image_emb, text_emb, positives, pair_mask, log_scale, bias)
    parts, tiles = 6, 3
    places = block_count // 2
    groups = lax.axis_size("grp")
    smem = pl.BlockSpec(memory_space=pltpu.SMEM)
    anywhere = pl.BlockSpec(memory_space=pl.ANY)
    column = places * row_count
    return pl.pallas_call(
        functools.partial(grid_kernel, reach, parts, tiles),
        out_shape=(
            jax.ShapeDtypeStruct(image_emb.shape, image_emb.dtype),
            jax.ShapeDtypeStruct(text_emb.shape, text_emb.dtype),
            jax.ShapeDtypeStruct((1,), jnp.float32),
        ),
        in_specs=[smem] * 3 + [anywhere] * 3,
        out_specs=(anywhere, anywhere, smem),
        scratch_shapes=[
            pltpu.VMEM((column, width), jnp.bfloat16),
            pltpu.VMEM((2, row_count, width), jnp.bfloat16),
            pltpu.VMEM((1, row_count), jnp.int32),
            pltpu.VMEM((column, width), jnp.bfloat16),
            pltpu.VMEM((2 * row_count, width), jnp.bfloat16),
            pltpu.VMEM((1 + tiles, row_count, row_count // tiles), jnp.float32),
            pltpu.VMEM((2, row_count, column), jnp.bfloat16),
            pltpu.VMEM((column, width), jnp.float32),
            pltpu.VMEM((column, width), jnp.bfloat16),
            pltpu.VMEM((2, column, width), jnp.bfloat16),
            pltpu.VMEM((row_count, width), jnp.float32),
            pltpu.VMEM((row_count, width), jnp.bfloat16),
            pltpu.VMEM((row_count, width), jnp.bfloat16),
            pltpu.VMEM((2, row_count, width), jnp.bfloat16),
            pltpu.VMEM((1, row_count // tiles), jnp.float32),
            pltpu.VMEM((block_count, 8, 128), jnp.float32),
            pltpu.VMEM((groups, 8, 128), jnp.float32),
            pltpu.SemaphoreType.DMA((3,)),
            pltpu.SemaphoreType.DMA((2, parts)),
            pltpu.SemaphoreType.DMA((3, 4, parts)),
            pltpu.SemaphoreType.DMA((places, parts)),
            pltpu.SemaphoreType.DMA((parts,)),
            pltpu.SemaphoreType.DMA((2, places, parts)),
            pltpu.SemaphoreType.DMA((parts,)),
            pltpu.SemaphoreType.DMA((block_count,)),
            pltpu.SemaphoreType.DMA((block_count,)),
            pltpu.SemaphoreType.DMA((groups,)),
            pltpu.SemaphoreType.DMA((groups,)),
        ],
        compiler_params=pltpu.CompilerParams(
            collective_id=0, has_side_effects=True, vmem_limit_bytes=67043328
        ),
    )(pair_mask, log_scale, bias, image_emb, text_emb, positives)


def solution(mesh):
    return jax.shard_map(
        body,
        mesh=mesh,
        in_specs=(
            P(("blk", "grp"), None),
            P(("blk", "grp"), None),
            P(("blk", "grp"), None),
            P(),
            P(),
            P(),
        ),
        out_specs=(P(("blk", "grp"), None), P(("blk", "grp"), None), P()),
        check_vma=False,
    )
```

time: 144 us -> 101 us (0.70)
  Pallas kernels: 137 us -> 93.7 us
    pallas_call x1, Pallas kernels: 137 us -> 93.7 us  [body(): pl.pallas_call(functools.partial(grid_kernel, reach, parts, tiles), out_s...]
where the time goes in v1:
time: 101 us
  Pallas kernels  93.7 us (93%)
  between operations  3.76 us (4%)
  local copies, waits for them, and re-layouts  3.14 us (3%)
    pallas_call x1, Pallas kernels, body(): pl.pallas_call(functools.partial(grid_kernel, reach, parts, tiles), out_s...  93.7 us
    unnamed x4, local copies, waits for them, and re-layouts  3.14 us

profile of v1, /device:TPU:0, one launch (start us, length us, event | category | flops | bytes accessed | tf_op | source)
XLA Modules:
  0.0 100.6 jit_solution(4418958571028502898)
XLA Ops:
  1.9 93.7 %shard_map.85 = (bf16[384,1152]{1,0:T(8,128)(2,1)}, bf16[384,1152]{1,0:T(8,128)(2,1)}, f32[1]{0:T(128)}) custom-call(s32[8,7]{1,0:T(8,128)} %mask_ref.1, f32[1]{0:T(128)S(6)} %copy.12.scale_ref, f32[1]{0:T(128)S(6)} %copy.13.offset_ref, bf16[384,1152]{1,0:T(8,128)(2,1)} %image_hbm.1, bf16[384,1152]{1,0:T(8,128)(2,1)} %text_hbm.1, s32[1,384]{1,0:T(1,128)} %pos_hbm.1), custom_call_target="tpu_custom_call" | custom-call | tf_op jit(solution)/shard_map/pallas_call | solution.py:442
  95.7 0.0 copy-start
  95.7 2.2 %copy.14 = bf16[384,1152]{1,0:T(8,128)(2,1)} copy(bf16[384,1152]{1,0:T(8,128)(2,1)} %get-tuple-element.6) | data formatting | bytes 1769472
  97.9 0.0 copy-done
  97.9 0.9 copy.15
Async XLA Ops:
  95.7 2.2 %copy-start = (bf16[384,1152]{1,0:T(8,128)(2,1)S(1)}, bf16[384,1152]{1,0:T(8,128)(2,1)}, u32[]{:S(2)}) copy-start(bf16[384,1152]{1,0:T(8,128)(2,1)} %get-tuple-element.7) | copy-start | bytes 2654212

commit v2 on v1

--- a/solution.py
+++ b/solution.py
@@ -103,12 +103,13 @@
 OWN, OTHER = 0, 1
 
 
-def grid_kernel(reach, parts, tiles, mask_ref, scale_ref, offset_ref, image_hbm, text_hbm, pos_hbm,
+def grid_kernel(reach, parts, tiles, mask_hbm, scale_hbm, offset_hbm, image_hbm, text_hbm, pos_hbm,
                 image_out, text_out, loss_out,
+                mask_ref, scale_ref, offset_ref, loss_ref,
                 texts, images, pos_row, unit_texts, unit_images, labels, slopes, terms, sent, got,
-                image_acc, image_sent, image_got, ready, loss_acc, blk_loss, grp_loss,
-                load_sem, out_sem, send_sem, text_recv, image_recv, term_recv, back_recv,
-                blk_send, blk_recv, grp_send, grp_recv):
+                image_acc, image_sent, image_got, loss_acc, line_loss, plane_loss,
+                load_sem, send_sem, text_recv, image_recv, term_recv, back_recv,
+                line_send, line_recv, plane_send, plane_recv):
     me = lax.axis_index("blk")
     grp = lax.axis_index("grp")
     count = lax.axis_size("blk")
@@ -140,69 +141,82 @@
     def tile_at(which, c):
         return pl.ds(pl.multiple_of(which * rows + c * tall, tall), tall)
 
-    def send(way, slot, c, source, target, recv):
+    def send(way, slot, source, target, recv):
         return pltpu.make_async_remote_copy(
-            src_ref=source, dst_ref=target, send_sem=send_sem.at[way, slot, c], recv_sem=recv,
+            src_ref=source, dst_ref=target, send_sem=send_sem.at[way, slot], recv_sem=recv,
             device_id=(targets[way], grp), device_id_type=MESH)
 
     def text_copy(way, slot, which, c):
-        return send(way, slot, c, texts.at[at(which, c)], texts.at[at(which, c)], text_recv.at[which, c])
+        return send(way, slot, texts.at[at(which, c)], texts.at[at(which, c)], text_recv.at[which, c])
 
     def image_copy(c):
-        return send(Y, 0, c, images.at[OWN, cut(c)], images.at[OTHER, cut(c)], image_recv.at[c])
+        return send(Y, 0, images.at[OWN, cut(c)], images.at[OTHER, cut(c)], image_recv.at[c])
 
     def back_copy(c):
-        return send(Y, 1, c, image_sent.at[cut(c)], image_got.at[cut(c)], back_recv.at[c])
-
-    def term_copy(way, slot, which, side, c):
-        return send(way, slot, c, sent.at[at(which, c)], got.at[side, at(which, c)], term_recv.at[side, which, c])
-
-    def term_arrived(side, which, c):
-        term_copy(INNER, 0, which, side, c).wait_recv()
+        return send(Y, 1, image_sent.at[cut(c)], image_got.at[cut(c)], back_recv.at[c])
+
+    def term_copy(way, slot, which, kind, c):
+        return send(way, slot, sent.at[at(which, c)], got.at[kind, cut(c)], term_recv.at[kind, c])
+
+    def term_arrived(kind, c):
+        term_copy(INNER, 0, 0, kind, c).wait_recv()
+
+    def all_sent(way, slot):
+        block = texts.at[pl.ds(0, rows)]
+        send(way, slot, block, block, text_recv.at[0, 0]).wait_send()
 
     own_row = place_row(role)
     loads = [
-        pltpu.make_async_copy(text_hbm, texts.at[pl.ds(pl.multiple_of(own_row * rows, rows), rows)], load_sem.at[0]),
-        pltpu.make_async_copy(image_hbm, images.at[OWN], load_sem.at[1]),
-        pltpu.make_async_copy(pos_hbm, pos_row, load_sem.at[2]),
+        pltpu.make_async_copy(source, target, load_sem.at[i])
+        for i, (source, target) in enumerate((
+            (text_hbm, texts.at[pl.ds(pl.multiple_of(own_row * rows, rows), rows)]),
+            (image_hbm, images.at[OWN]), (pos_hbm, pos_row),
+            (mask_hbm, mask_ref), (scale_hbm, scale_ref), (offset_hbm, offset_ref)))
     ]
     for load in loads:
         load.start()
     barrier = pltpu.get_barrier_semaphore()
-
-    @pl.loop(1, count)
+    plane = 2 * groups
+    spot = col * groups + grp
+
+    def in_plane(d):
+        other = lax.rem(spot + d, plane)
+        return other, (row * 2 + other // groups, lax.rem(other, groups))
+
+    pl.semaphore_signal(barrier, inc=1, device_id=(inner, grp), device_id_type=MESH)
+
+    @pl.when(is_mid)
+    def _():
+        pl.semaphore_signal(barrier, inc=1, device_id=(outer, grp), device_id_type=MESH)
+
+    @pl.loop(1, plane)
     def _(d):
-        pl.semaphore_signal(barrier, inc=1, device_id=(lax.rem(me + d, count), grp), device_id_type=MESH)
-
-    @pl.loop(1, groups)
-    def _(d):
-        pl.semaphore_signal(barrier, inc=1, device_id=(me, lax.rem(grp + d, groups)), device_id_type=MESH)
-
-    pl.semaphore_wait(barrier, count + groups - 2)
-
-    def blk_share(d):
-        target = lax.rem(me + d, count)
+        pl.semaphore_signal(barrier, inc=1, device_id=in_plane(d)[1], device_id_type=MESH)
+
+    pl.semaphore_wait(barrier, plane + role)
+
+    def line_share(d):
+        target = lax.rem(row + d, places)
         return pltpu.make_async_remote_copy(
-            src_ref=blk_loss.at[me], dst_ref=blk_loss.at[me], send_sem=blk_send.at[d],
-            recv_sem=blk_recv.at[me], device_id=(target, grp), device_id_type=MESH)
-
-    def blk_arrival(d):
-        source = lax.rem(me + d, count)
+            src_ref=line_loss.at[row], dst_ref=line_loss.at[row], send_sem=line_send.at[0],
+            recv_sem=line_recv.at[row], device_id=(target * 2 + col, grp), device_id_type=MESH)
+
+    def line_arrival(d):
+        source = lax.rem(row + d, places)
         return pltpu.make_async_remote_copy(
-            src_ref=blk_loss.at[source], dst_ref=blk_loss.at[source], send_sem=blk_send.at[d],
-            recv_sem=blk_recv.at[source], device_id=(source, grp), device_id_type=MESH)
-
-    def grp_share(d):
-        target = lax.rem(grp + d, groups)
+            src_ref=line_loss.at[source], dst_ref=line_loss.at[source], send_sem=line_send.at[0],
+            recv_sem=line_recv.at[source], device_id=(source * 2 + col, grp), device_id_type=MESH)
+
+    def plane_share(d):
         return pltpu.make_async_remote_copy(
-            src_ref=grp_loss.at[grp], dst_ref=grp_loss.at[grp], send_sem=grp_send.at[d],
-            recv_sem=grp_recv.at[grp], device_id=(me, target), device_id_type=MESH)
-
-    def grp_arrival(d):
-        source = lax.rem(grp + d, groups)
+            src_ref=plane_loss.at[spot], dst_ref=plane_loss.at[spot], send_sem=plane_send.at[0],
+            recv_sem=plane_recv.at[spot], device_id=in_plane(d)[1], device_id_type=MESH)
+
+    def plane_arrival(d):
+        other, device = in_plane(d)
         return pltpu.make_async_remote_copy(
-            src_ref=grp_loss.at[source], dst_ref=grp_loss.at[source], send_sem=grp_send.at[d],
-            recv_sem=grp_recv.at[source], device_id=(me, source), device_id_type=MESH)
+            src_ref=plane_loss.at[other], dst_ref=plane_loss.at[other], send_sem=plane_send.at[0],
+            recv_sem=plane_recv.at[other], device_id=device, device_id_type=MESH)
 
     loads[0].wait()
 
@@ -220,6 +234,9 @@
     def _(c):
         image_copy(c).start()
 
+    for load in loads[2:]:
+        load.wait()
+
     scale = jnp.exp(jnp.full((1, 1), scale_ref[0], jnp.float32))
     offset = jnp.full((1, 1), offset_ref[0], jnp.float32)
 
@@ -228,7 +245,6 @@
         return values / length, length
 
     loss_acc[...] = jnp.zeros_like(loss_acc)
-    loads[2].wait()
 
     @pl.loop(0, tiles)
     def _(c):
@@ -283,12 +299,12 @@
         terms[tile_at(which, c), :] = term
         sent[tile_at(which, c), :] = term.astype(jnp.bfloat16)
 
-    def relay(way, slot, side, p, c):
+    def relay(way, slot, kind, p, onward, c):
         which = place_row(p)
-        term_arrived(side, which, c)
-        total = terms[at(which, c), :] + got[side, at(which, c), :].astype(jnp.float32)
+        term_arrived(kind, c)
+        total = terms[at(which, c), :] + got[kind, cut(c), :].astype(jnp.float32)
         sent[at(which, c), :] = total.astype(jnp.bfloat16)
-        term_copy(way, slot, which, 1, c).start()
+        term_copy(way, slot, which, onward, c).start()
 
     steps = 4 * tiles
 
@@ -317,34 +333,36 @@
 
         item(p, which, c)
 
+        @pl.when(s == steps - 1)
+        def _():
+            line_loss[row] = jnp.full(line_loss.shape[1:], jnp.sum(loss_acc[...]), jnp.float32)
+
+            @pl.loop(1, places)
+            def _(d):
+                line_share(d).start()
+
         @pl.when((1 - role) * p * (p // 3 + (tiles - c) // 2) > 0)
         def _():
             @pl.loop(0, per_tile)
             def _(k):
-                term_copy(INNER, p, which, 0, c * per_tile + k).start()
+                term_copy(INNER, p, which, p - 1, c * per_tile + k).start()
 
         @pl.when(role * (s // 7) * (1 - s // 11) == 1)
         def _():
-            relay(INNER, 2, 0, 2, s - 7)
+            relay(INNER, 2, 1, 2, 3, s - 7)
 
     @pl.when(is_end)
     def _():
         @pl.loop(0, 2 * per_tile)
         def _(k):
             p = 2 - k // per_tile
-            term_copy(INNER, p, place_row(p), 0, parts - per_tile + k % per_tile).start()
-
-    blk_loss[me] = jnp.full(blk_loss.shape[1:], jnp.sum(loss_acc[...]), jnp.float32)
-
-    @pl.loop(1, count)
-    def _(d):
-        blk_share(d).start()
+            term_copy(INNER, p, place_row(p), p - 1, parts - per_tile + k % per_tile).start()
 
     @pl.loop(0, parts)
     def _(c):
         @pl.when(is_mid)
         def _():
-            relay(INNER, 3, 0, 3, c)
+            relay(INNER, 3, 2, 3, 4, c)
 
         whole = jnp.dot(slopes[OTHER, cut(c), :], unit_texts[...], preferred_element_type=jnp.float32)
         image_sent[cut(c), :] = whole.astype(jnp.bfloat16)
@@ -354,77 +372,90 @@
 
         @pl.when(role * c > 0)
         def _():
-            relay(OUTER, 3, 1, 0, c - 1)
+            relay(OUTER, 3, 4, 0, 3, c - 1)
+
+        @pl.when(c == parts - 1)
+        def _():
+            @pl.loop(1, places)
+            def _(d):
+                line_arrival(d).wait_recv()
+
+            plane_loss[spot] = jnp.sum(line_loss[...], axis=0)
+
+            @pl.loop(1, plane)
+            def _(d):
+                plane_share(d).start()
 
     @pl.when(is_mid)
     def _():
-        relay(OUTER, 3, 1, 0, parts - 1)
+        relay(OUTER, 3, 4, 0, 3, parts - 1)
 
         @pl.loop(parts - per_tile, parts)
         def _(c):
-            relay(INNER, 2, 0, 2, c)
-
-    @pl.loop(1, count)
-    def _(d):
-        blk_arrival(d).wait_recv()
-
-    grp_loss[grp] = jnp.sum(blk_loss[...], axis=0)
-
-    @pl.loop(1, groups)
-    def _(d):
-        grp_share(d).start()
-
-    def put_out(side, result, c):
-        return pltpu.make_async_copy(ready.at[side, cut(c)], result.at[cut(c)], out_sem.at[side, c])
-
-    def finish(side, source, upstream, result, c):
+            relay(INNER, 2, 1, 2, 3, c)
+
+    def put_loss():
+        return pltpu.make_async_copy(loss_ref, loss_out, load_sem.at[0])
+
+    def finish(source, upstream, result, c):
         normed, length = unit(source.astype(jnp.float32))
-        ready[side, cut(c), :] = back_rows(normed, length, upstream).astype(ready.dtype)
-        put_out(side, result, c).start()
+        result[cut(c), :] = back_rows(normed, length, upstream).astype(result.dtype)
 
     @pl.loop(0, parts)
     def _(c):
-        term_arrived(1, own_row, c)
+        @pl.when(c == parts // 2)
+        def _():
+            @pl.loop(1, plane)
+            def _(d):
+                plane_arrival(d).wait_recv()
+
+            total = jnp.sum(plane_loss[...], axis=0)
+            loss_ref[0] = jnp.sum(total[0:1, 0:1]) / (rows * count * groups)
+            put_loss().start()
 
         @pl.when(is_mid)
         def _():
-            term_arrived(0, own_row, c)
-            terms[at(own_row, c), :] += got[0, at(own_row, c), :].astype(jnp.float32)
-
-        total = terms[at(own_row, c), :] + got[1, at(own_row, c), :].astype(jnp.float32)
-        finish(1, texts[at(own_row, c), :], total, text_out, c)
+            term_arrived(0, c)
+            terms[at(own_row, c), :] += got[0, cut(c), :].astype(jnp.float32)
+
+        term_arrived(3, c)
+        total = terms[at(own_row, c), :] + got[3, cut(c), :].astype(jnp.float32)
+        finish(texts[at(own_row, c), :], total, text_out, c)
         back_copy(c).wait_recv()
         total = image_acc[cut(c), :] + image_got[cut(c), :].astype(jnp.float32)
-        finish(0, images[OWN, cut(c), :], total, image_out, c)
-
-    @pl.loop(1, groups)
-    def _(d):
-        grp_arrival(d).wait_recv()
-
-    total = jnp.sum(grp_loss[...], axis=0)
-    loss_out[0] = jnp.sum(total[0:1, 0:1]) / (rows * count * groups)
-
-    @pl.loop(1, count)
-    def _(d):
-        blk_share(d).wait_send()
-
-    @pl.loop(1, groups)
-    def _(d):
-        grp_share(d).wait_send()
-
-    @pl.loop(0, parts)
-    def _(c):
-        put_out(0, image_out, c).wait()
-        put_out(1, text_out, c).wait()
-        for slot in range(2):
-            text_copy(Y, slot, own_row, c).wait_send()
+        finish(images[OWN, cut(c), :], total, image_out, c)
+
+    put_loss().wait()
+    lines = line_loss.at[pl.ds(0, places - 1)]
+    pltpu.make_async_remote_copy(
+        src_ref=lines, dst_ref=lines, send_sem=line_send.at[0], recv_sem=line_recv.at[0],
+        device_id=(inner, grp), device_id_type=MESH).wait_send()
+    planes = plane_loss.at[pl.ds(0, plane - 1)]
+    pltpu.make_async_remote_copy(
+        src_ref=planes, dst_ref=planes, send_sem=plane_send.at[0], recv_sem=plane_recv.at[0],
+        device_id=(inner, grp), device_id_type=MESH).wait_send()
+    for slot in range(2):
+        all_sent(Y, slot)
+    for slot in range(4):
+        all_sent(INNER, slot)
+
+    @pl.when(is_mid)
+    def _():
         for slot in range(4):
-            text_copy(INNER, slot, own_row, c).wait_send()
-
-        @pl.when(is_mid)
-        def _():
-            for slot in range(4):
-                text_copy(OUTER, slot, own_row, c).wait_send()
+            all_sent(OUTER, slot)
+
+
+def store_kernel(pieces, image_ref, text_ref, image_out, text_out, sem):
+    height = image_ref.shape[0] // pieces
+    copies = [
+        pltpu.make_async_copy(source.at[pl.ds(c * height, height)], result.at[pl.ds(c * height, height)], sem.at[i, c])
+        for i, (source, result) in enumerate(((image_ref, image_out), (text_ref, text_out)))
+        for c in range(pieces)
+    ]
+    for copy in copies:
+        copy.start()
+    for copy in copies:
+        copy.wait()
 
 
 def body(image_emb, text_emb, positives, pair_mask, log_scale, bias):
@@ -436,19 +467,24 @@
     parts, tiles = 6, 3
     places = block_count // 2
     groups = lax.axis_size("grp")
-    smem = pl.BlockSpec(memory_space=pltpu.SMEM)
+    vmem = pl.BlockSpec(memory_space=pltpu.VMEM)
     anywhere = pl.BlockSpec(memory_space=pl.ANY)
     column = places * row_count
-    return pl.pallas_call(
+    grant = 67043328 - 2 * image_emb.size * image_emb.dtype.itemsize
+    image_grad, text_grad, loss = pl.pallas_call(
         functools.partial(grid_kernel, reach, parts, tiles),
         out_shape=(
-            jax.ShapeDtypeStruct(image_emb.shape, image_emb.dtype),
-            jax.ShapeDtypeStruct(text_emb.shape, text_emb.dtype),
+            pltpu.VMEM(image_emb.shape, image_emb.dtype),
+            pltpu.VMEM(text_emb.shape, text_emb.dtype),
             jax.ShapeDtypeStruct((1,), jnp.float32),
         ),
-        in_specs=[smem] * 3 + [anywhere] * 3,
-        out_specs=(anywhere, anywhere, smem),
+        in_specs=[pl.BlockSpec(memory_space=pltpu.HBM)] * 6,
+        out_specs=(vmem, vmem, anywhere),
         scratch_shapes=[
+            pltpu.SMEM(pair_mask.shape, jnp.int32),
+            pltpu.SMEM((1,), jnp.float32),
+            pltpu.SMEM((1,), jnp.float32),
+            pltpu.SMEM((1,), jnp.float32),
             pltpu.VMEM((column, width), jnp.bfloat16),
             pltpu.VMEM((2, row_count, width), jnp.bfloat16),
             pltpu.VMEM((1, row_count), jnp.int32),
@@ -458,30 +494,41 @@
             pltpu.VMEM((2, row_count, column), jnp.bfloat16),
             pltpu.VMEM((column, width), jnp.float32),
             pltpu.VMEM((column, width), jnp.bfloat16),
-            pltpu.VMEM((2, column, width), jnp.bfloat16),
+            pltpu.VMEM((5, row_count, width), jnp.bfloat16),
             pltpu.VMEM((row_count, width), jnp.float32),
             pltpu.VMEM((row_count, width), jnp.bfloat16),
             pltpu.VMEM((row_count, width), jnp.bfloat16),
-            pltpu.VMEM((2, row_count, width), jnp.bfloat16),
             pltpu.VMEM((1, row_count // tiles), jnp.float32),
-            pltpu.VMEM((block_count, 8, 128), jnp.float32),
-            pltpu.VMEM((groups, 8, 128), jnp.float32),
-            pltpu.SemaphoreType.DMA((3,)),
-            pltpu.SemaphoreType.DMA((2, parts)),
-            pltpu.SemaphoreType.DMA((3, 4, parts)),
+            pltpu.VMEM((places, 8, 128), jnp.float32),
+            pltpu.VMEM((2 * groups, 8, 128), jnp.float32),
+            pltpu.SemaphoreType.DMA((6,)),
+            pltpu.SemaphoreType.DMA((3, 4)),
             pltpu.SemaphoreType.DMA((places, parts)),
             pltpu.SemaphoreType.DMA((parts,)),
-            pltpu.SemaphoreType.DMA((2, places, parts)),
+            pltpu.SemaphoreType.DMA((5, parts)),
             pltpu.SemaphoreType.DMA((parts,)),
-            pltpu.SemaphoreType.DMA((block_count,)),
-            pltpu.SemaphoreType.DMA((block_count,)),
-            pltpu.SemaphoreType.DMA((groups,)),
-            pltpu.SemaphoreType.DMA((groups,)),
+            pltpu.SemaphoreType.DMA((1,)),
+            pltpu.SemaphoreType.DMA((places,)),
+            pltpu.SemaphoreType.DMA((1,)),
+            pltpu.SemaphoreType.DMA((2 * groups,)),
         ],
         compiler_params=pltpu.CompilerParams(
-            collective_id=0, has_side_effects=True, vmem_limit_bytes=67043328
+            collective_id=0, has_side_effects=True, vmem_limit_bytes=grant
         ),
     )(pair_mask, log_scale, bias, image_emb, text_emb, positives)
+    pieces = 4
+    image_grad, text_grad = pl.pallas_call(
+        functools.partial(store_kernel, pieces),
+        out_shape=(
+            jax.ShapeDtypeStruct(image_emb.shape, image_emb.dtype),
+            jax.ShapeDtypeStruct(text_emb.shape, text_emb.dtype),
+        ),
+        in_specs=[vmem] * 2,
+        out_specs=[pl.BlockSpec(memory_space=pltpu.HBM)] * 2,
+        scratch_shapes=[pltpu.SemaphoreType.DMA((2, pieces))],
+        compiler_params=pltpu.CompilerParams(vmem_limit_bytes=4 * 1024 * 1024),
+    )(image_grad, text_grad)
+    return image_grad, text_grad, loss
 
 
 def solution(mesh):

time: 101 us -> 93.7 us (0.928)
  Pallas kernels: 93.7 us -> 89.8 us
  local copies, waits for them, and re-layouts: 3.14 us -> 0 us
    pallas_call x1, Pallas kernels: 93.7 us -> 88.6 us  [body(): pl.pallas_call(functools.partial(grid_kernel, reach, parts, tiles), out_s...]
    unnamed x4 -> x0, local copies, waits for them, and re-layouts: 3.14 us -> none
    pallas_call x0 -> x1, Pallas kernels: none -> 1.27 us  [body(): pl.pallas_call(functools.partial(store_kernel, pieces), out_shape=(jax.Sh...]
where the time goes in v2:
time: 93.7 us; the launch traced here: 93.5 us
  Pallas kernels  89.8 us (96%)
  between operations  3.7 us (4%)
    pallas_call x1, Pallas kernels, body(): pl.pallas_call(functools.partial(grid_kernel, reach, parts, tiles), out_s...  88.6 us

profile of v2, /device:TPU:0, one launch (start us, length us, event | category | flops | bytes accessed | tf_op | source)
XLA Modules:
  0.0 93.5 jit_solution(17017098872623636204)
XLA Ops:
  1.9 88.6 %shard_map.85 = (bf16[384,1152]{1,0:T(8,128)(2,1)S(1)}, bf16[384,1152]{1,0:T(8,128)(2,1)S(1)}, f32[1]{0:T(128)}) custom-call(s32[8,7]{1,0:T(8,128)} %mask_hbm.1, f32[1]{0:T(128)S(6)} %copy.10.scale_hbm, f32[1]{0:T(128)S(6)} %copy.11.offset_hbm, bf16[384,1152]{1,0:T(8,128)(2,1)} %image_hbm.1, bf16[384,1152]{1,0:T(8,128)(2,1)} %text_hbm.1, s32[1,384]{1,0:T(1,128)} %pos_hbm.1), custom_call_target="tpu_custom_call" | custom-call | tf_op jit(solution)/shard_map/pallas_call | solution.py:474
  90.5 1.3 %shard_map.86 = (bf16[384,1152]{1,0:T(8,128)(2,1)}, bf16[384,1152]{1,0:T(8,128)(2,1)}) custom-call(bf16[384,1152]{1,0:T(8,128)(2,1)S(1)} %get-tuple-element.8.image_ref, bf16[384,1152]{1,0:T(8,128)(2,1)S(1)} %get-tuple-element.9.text_ref), custom_call_target="tpu_custom_call" | custom-call | tf_op jit(solution)/shard_map/pallas_call | solution.py:520

commit v3 on v2

--- a/solution.py
+++ b/solution.py
@@ -107,7 +107,7 @@
                 image_out, text_out, loss_out,
                 mask_ref, scale_ref, offset_ref, loss_ref,
                 texts, images, pos_row, unit_texts, unit_images, labels, slopes, terms, sent, got,
-                image_acc, image_sent, image_got, loss_acc, line_loss, plane_loss,
+                image_acc, image_part, image_sent, image_got, loss_acc, line_loss, plane_loss,
                 load_sem, send_sem, text_recv, image_recv, term_recv, back_recv,
                 line_send, line_recv, plane_send, plane_recv):
     me = lax.axis_index("blk")
@@ -219,20 +219,7 @@
             recv_sem=plane_recv.at[other], device_id=device, device_id_type=MESH)
 
     loads[0].wait()
-
-    @pl.loop(0, parts)
-    def _(c):
-        text_copy(INNER, 0, own_row, c).start()
-
-        @pl.when(is_mid)
-        def _():
-            text_copy(OUTER, 0, own_row, c).start()
-
     loads[1].wait()
-
-    @pl.loop(0, parts)
-    def _(c):
-        image_copy(c).start()
 
     for load in loads[2:]:
         load.wait()
@@ -244,16 +231,58 @@
         length = jnp.sqrt(jnp.sum(values * values, axis=1, keepdims=True) + epsilon)
         return values / length, length
 
-    loss_acc[...] = jnp.zeros_like(loss_acc)
-
-    @pl.loop(0, tiles)
-    def _(c):
-        band = pl.ds(pl.multiple_of(c * tall, tall), tall)
-        unit_images[band, :] = unit(images[OWN, band, :].astype(jnp.float32))[0].astype(jnp.bfloat16)
-        hit = pos_row[...] == lax.broadcasted_iota(jnp.int32, (tall, rows), 0) + c * tall
-        labels[1 + c] = jnp.transpose(jnp.where(hit, -1.0, 1.0))
-
-    labels[0] = jnp.full(labels.shape[1:], 1.0, jnp.float32)
+    last_tile = tile_at(place_row(3 - 2 * role), tiles - 1)
+
+    def prepare():
+        loss_acc[...] = jnp.zeros_like(loss_acc)
+
+        @pl.loop(0, tiles)
+        def _(c):
+            band = pl.ds(pl.multiple_of(c * tall, tall), tall)
+            unit_images[band, :] = unit(images[OWN, band, :].astype(jnp.float32))[0].astype(jnp.bfloat16)
+            hit = pos_row[...] == lax.broadcasted_iota(jnp.int32, (tall, rows), 0) + c * tall
+            labels[1 + c] = jnp.transpose(jnp.where(hit, -1.0, 1.0))
+
+        slopes[OTHER, :, last_tile] = jnp.zeros((rows, tall), jnp.bfloat16)
+        unit_texts[last_tile, :] = jnp.zeros((tall, texts.shape[1]), jnp.bfloat16)
+        labels[0] = jnp.full(labels.shape[1:], 1.0, jnp.float32)
+
+    second = lax.rem(grp, 2)
+
+    held = 1
+
+    def image_arrived(c):
+        image_copy(c).wait_recv()
+        unit_images[at(1, c), :] = unit(images[OTHER, cut(c), :].astype(jnp.float32))[0].astype(jnp.bfloat16)
+
+    def send_texts():
+        @pl.loop(0, parts)
+        def _(c):
+            text_copy(INNER, 0, own_row, c).start()
+
+            @pl.when(is_mid)
+            def _():
+                text_copy(OUTER, 0, own_row, c).start()
+
+    def send_images():
+        @pl.loop(0, parts)
+        def _(c):
+            image_copy(c).start()
+
+    @pl.when(second == 0)
+    def _():
+        send_texts()
+
+    send_images()
+    prepare()
+
+    @pl.when(second == 1)
+    def _():
+        @pl.loop(0, held)
+        def _(c):
+            image_arrived(c)
+
+        send_texts()
 
     @pl.loop(0, parts)
     def _(c):
@@ -264,8 +293,9 @@
             text_copy(Y, 0, place_row(2), c).wait_recv()
             text_copy(OUTER, 1, place_row(2), c).start()
 
-        image_copy(c).wait_recv()
-        unit_images[at(1, c), :] = unit(images[OTHER, cut(c), :].astype(jnp.float32))[0].astype(jnp.bfloat16)
+        @pl.when(c // held + (1 - second) > 0)
+        def _():
+            image_arrived(c)
 
     def flag_of(other, which):
         image = row * 2 + col + other * (1 - 2 * col)
@@ -318,6 +348,14 @@
         c = first * s + last * (s - 3 * tiles) + between * ((s + 1) // 2 - 2)
         which = place_row(p)
 
+        @pl.when(s == steps - 1)
+        def _():
+            @pl.loop(0, tiles)
+            def _(k):
+                band = pl.ds(pl.multiple_of(k * tall, tall), tall)
+                image_part[band, :] = jnp.dot(
+                    slopes[OTHER, band, :], unit_texts[...], preferred_element_type=jnp.float32)
+
         @pl.when((1 - role) * p > 0)
         def _():
             @pl.loop(0, per_tile)
@@ -341,22 +379,21 @@
             def _(d):
                 line_share(d).start()
 
-        @pl.when((1 - role) * p * (p // 3 + (tiles - c) // 2) > 0)
+        @pl.when((1 - role) * (p // 2 + p % 2 * ((tiles - c) // tiles)) > 0)
         def _():
             @pl.loop(0, per_tile)
             def _(k):
                 term_copy(INNER, p, which, p - 1, c * per_tile + k).start()
 
-        @pl.when(role * (s // 7) * (1 - s // 11) == 1)
-        def _():
-            relay(INNER, 2, 1, 2, 3, s - 7)
+        @pl.when(role * (s // 6) * (1 - s // 11) == 1)
+        def _():
+            relay(INNER, 2, 1, 2, 3, s - 6)
 
     @pl.when(is_end)
     def _():
-        @pl.loop(0, 2 * per_tile)
+        @pl.loop(per_tile, parts)
         def _(k):
-            p = 2 - k // per_tile
-            term_copy(INNER, p, place_row(p), p - 1, parts - per_tile + k % per_tile).start()
+            term_copy(INNER, 1, place_row(1), 0, k).start()
 
     @pl.loop(0, parts)
     def _(c):
@@ -364,7 +401,8 @@
         def _():
             relay(INNER, 3, 2, 3, 4, c)
 
-        whole = jnp.dot(slopes[OTHER, cut(c), :], unit_texts[...], preferred_element_type=jnp.float32)
+        whole = image_part[cut(c), :] + jnp.dot(
+            slopes[OTHER, cut(c), last_tile], unit_texts[last_tile, :], preferred_element_type=jnp.float32)
         image_sent[cut(c), :] = whole.astype(jnp.bfloat16)
         back_copy(c).start()
         image_acc[cut(c), :] = jnp.dot(
@@ -390,9 +428,7 @@
     def _():
         relay(OUTER, 3, 4, 0, 3, parts - 1)
 
-        @pl.loop(parts - per_tile, parts)
-        def _(c):
-            relay(INNER, 2, 1, 2, 3, c)
+        relay(INNER, 2, 1, 2, 3, parts - 1)
 
     def put_loss():
         return pltpu.make_async_copy(loss_ref, loss_out, load_sem.at[0])
@@ -496,6 +532,7 @@
             pltpu.VMEM((column, width), jnp.bfloat16),
             pltpu.VMEM((5, row_count, width), jnp.bfloat16),
             pltpu.VMEM((row_count, width), jnp.float32),
+            pltpu.VMEM((row_count, width), jnp.float32),
             pltpu.VMEM((row_count, width), jnp.bfloat16),
             pltpu.VMEM((row_count, width), jnp.bfloat16),
             pltpu.VMEM((1, row_count // tiles), jnp.float32),

time: 93.7 us -> 92 us (0.982); the launches traced: 93.5 us -> 90.2 us
  Pallas kernels: 89.8 us -> 86.5 us
    pallas_call x1, Pallas kernels: 88.6 us -> 85.2 us  [body(): pl.pallas_call(functools.partial(grid_kernel, reach, parts, tiles), out_s...]
where the time goes in v3:
time: 92 us; the launch traced here: 90.2 us
  Pallas kernels  86.5 us (94%)
  between operations  3.7 us (4%)
    pallas_call x1, Pallas kernels, body(): pl.pallas_call(functools.partial(grid_kernel, reach, parts, tiles), out_s...  85.2 us

profile of v3, /device:TPU:0, one launch (start us, length us, event | category | flops | bytes accessed | tf_op | source)
XLA Modules:
  0.0 90.2 jit_solution(315474556489324080)
XLA Ops:
  1.9 85.2 %shard_map.85 = (bf16[384,1152]{1,0:T(8,128)(2,1)S(1)}, bf16[384,1152]{1,0:T(8,128)(2,1)S(1)}, f32[1]{0:T(128)}) custom-call(s32[8,7]{1,0:T(8,128)} %mask_hbm.1, f32[1]{0:T(128)S(6)} %copy.10.scale_hbm, f32[1]{0:T(128)S(6)} %copy.11.offset_hbm, bf16[384,1152]{1,0:T(8,128)(2,1)} %image_hbm.1, bf16[384,1152]{1,0:T(8,128)(2,1)} %text_hbm.1, s32[1,384]{1,0:T(1,128)} %pos_hbm.1), custom_call_target="tpu_custom_call" | custom-call | tf_op jit(solution)/shard_map/pallas_call | solution.py:510
  87.2 1.3 %shard_map.86 = (bf16[384,1152]{1,0:T(8,128)(2,1)}, bf16[384,1152]{1,0:T(8,128)(2,1)}) custom-call(bf16[384,1152]{1,0:T(8,128)(2,1)S(1)} %get-tuple-element.8.image_ref, bf16[384,1152]{1,0:T(8,128)(2,1)S(1)} %get-tuple-element.9.text_ref), custom_call_target="tpu_custom_call" | custom-call | tf_op jit(solution)/shard_map/pallas_call | solution.py:557

commit v4 on v3

--- a/solution.py
+++ b/solution.py
@@ -149,8 +149,11 @@
     def text_copy(way, slot, which, c):
         return send(way, slot, texts.at[at(which, c)], texts.at[at(which, c)], text_recv.at[which, c])
 
-    def image_copy(c):
-        return send(Y, 0, images.at[OWN, cut(c)], images.at[OTHER, cut(c)], image_recv.at[c])
+    def half_cut(i):
+        return pl.ds(pl.multiple_of(i * (piece // 2), piece // 2), piece // 2)
+
+    def image_copy(i):
+        return send(Y, 0, images.at[OWN, half_cut(i)], images.at[OTHER, half_cut(i)], image_recv.at[i])
 
     def back_copy(c):
         return send(Y, 1, image_sent.at[cut(c)], image_got.at[cut(c)], back_recv.at[c])
@@ -249,14 +252,15 @@
 
     second = lax.rem(grp, 2)
 
-    held = 1
-
-    def image_arrived(c):
-        image_copy(c).wait_recv()
-        unit_images[at(1, c), :] = unit(images[OTHER, cut(c), :].astype(jnp.float32))[0].astype(jnp.bfloat16)
-
-    def send_texts():
-        @pl.loop(0, parts)
+    early, held = 2, 5
+
+    def image_arrived(i):
+        image_copy(i).wait_recv()
+        there = pl.ds(pl.multiple_of(rows + i * (piece // 2), piece // 2), piece // 2)
+        unit_images[there, :] = unit(images[OTHER, half_cut(i), :].astype(jnp.float32))[0].astype(jnp.bfloat16)
+
+    def send_texts(first, last):
+        @pl.loop(first, last)
         def _(c):
             text_copy(INNER, 0, own_row, c).start()
 
@@ -264,16 +268,12 @@
             def _():
                 text_copy(OUTER, 0, own_row, c).start()
 
-    def send_images():
-        @pl.loop(0, parts)
-        def _(c):
-            image_copy(c).start()
-
-    @pl.when(second == 0)
-    def _():
-        send_texts()
-
-    send_images()
+    send_texts(0, parts - second * (parts - early))
+
+    @pl.loop(0, 2 * parts)
+    def _(i):
+        image_copy(i).start()
+
     prepare()
 
     @pl.when(second == 1)
@@ -282,7 +282,7 @@
         def _(c):
             image_arrived(c)
 
-        send_texts()
+        send_texts(early, parts)
 
     @pl.loop(0, parts)
     def _(c):
@@ -293,9 +293,11 @@
             text_copy(Y, 0, place_row(2), c).wait_recv()
             text_copy(OUTER, 1, place_row(2), c).start()
 
-        @pl.when(c // held + (1 - second) > 0)
-        def _():
-            image_arrived(c)
+        @pl.loop(2 * c, 2 * c + 2)
+        def _(i):
+            @pl.when(i // held + (1 - second) > 0)
+            def _():
+                image_arrived(i)
 
     def flag_of(other, which):
         image = row * 2 + col + other * (1 - 2 * col)
@@ -541,7 +543,7 @@
             pltpu.SemaphoreType.DMA((6,)),
             pltpu.SemaphoreType.DMA((3, 4)),
             pltpu.SemaphoreType.DMA((places, parts)),
-            pltpu.SemaphoreType.DMA((parts,)),
+            pltpu.SemaphoreType.DMA((2 * parts,)),
             pltpu.SemaphoreType.DMA((5, parts)),
             pltpu.SemaphoreType.DMA((parts,)),
             pltpu.SemaphoreType.DMA((1,)),

time: 92 us -> 90.9 us (0.988); the launches traced: 90.2 us -> 90.7 us
  no operation moved by 1% of the time
where the time goes in v4:
time: 90.9 us; the launch traced here: 90.7 us
  Pallas kernels  87 us (96%)
  between operations  3.7 us (4%)
    pallas_call x1, Pallas kernels, body(): pl.pallas_call(functools.partial(grid_kernel, reach, parts, tiles), out_s...  85.7 us

profile of v4, /device:TPU:0, one launch (start us, length us, event | category | flops | bytes accessed | tf_op | source)
XLA Modules:
  0.0 90.7 jit_solution(8168612343813165909)
XLA Ops:
  1.9 85.7 %shard_map.85 = (bf16[384,1152]{1,0:T(8,128)(2,1)S(1)}, bf16[384,1152]{1,0:T(8,128)(2,1)S(1)}, f32[1]{0:T(128)}) custom-call(s32[8,7]{1,0:T(8,128)} %mask_hbm.1, f32[1]{0:T(128)S(6)} %copy.10.scale_hbm, f32[1]{0:T(128)S(6)} %copy.11.offset_hbm, bf16[384,1152]{1,0:T(8,128)(2,1)} %image_hbm.1, bf16[384,1152]{1,0:T(8,128)(2,1)} %text_hbm.1, s32[1,384]{1,0:T(1,128)} %pos_hbm.1), custom_call_target="tpu_custom_call" | custom-call | tf_op jit(solution)/shard_map/pallas_call | solution.py:512
  87.7 1.3 %shard_map.86 = (bf16[384,1152]{1,0:T(8,128)(2,1)}, bf16[384,1152]{1,0:T(8,128)(2,1)}) custom-call(bf16[384,1152]{1,0:T(8,128)(2,1)S(1)} %get-tuple-element.8.image_ref, bf16[384,1152]{1,0:T(8,128)(2,1)S(1)} %get-tuple-element.9.text_ref), custom_call_target="tpu_custom_call" | custom-call | tf_op jit(solution)/shard_map/pallas_call | solution.py:559

commit v5 on v4

--- a/solution.py
+++ b/solution.py
@@ -172,10 +172,17 @@
     loads = [
         pltpu.make_async_copy(source, target, load_sem.at[i])
         for i, (source, target) in enumerate((
-            (text_hbm, texts.at[pl.ds(pl.multiple_of(own_row * rows, rows), rows)]),
             (image_hbm, images.at[OWN]), (pos_hbm, pos_row),
             (mask_hbm, mask_ref), (scale_hbm, scale_ref), (offset_hbm, offset_ref)))
     ]
+
+    def text_load(c):
+        return pltpu.make_async_copy(text_hbm.at[cut(c)], texts.at[at(own_row, c)], load_sem.at[len(loads) + c])
+
+    @pl.loop(0, parts)
+    def _(c):
+        text_load(c).start()
+
     for load in loads:
         load.start()
     barrier = pltpu.get_barrier_semaphore()
@@ -220,15 +227,6 @@
         return pltpu.make_async_remote_copy(
             src_ref=plane_loss.at[other], dst_ref=plane_loss.at[other], send_sem=plane_send.at[0],
             recv_sem=plane_recv.at[other], device_id=device, device_id_type=MESH)
-
-    loads[0].wait()
-    loads[1].wait()
-
-    for load in loads[2:]:
-        load.wait()
-
-    scale = jnp.exp(jnp.full((1, 1), scale_ref[0], jnp.float32))
-    offset = jnp.full((1, 1), offset_ref[0], jnp.float32)
 
     def unit(values):
         length = jnp.sqrt(jnp.sum(values * values, axis=1, keepdims=True) + epsilon)
@@ -262,6 +260,7 @@
     def send_texts(first, last):
         @pl.loop(first, last)
         def _(c):
+            text_load(c).wait()
             text_copy(INNER, 0, own_row, c).start()
 
             @pl.when(is_mid)
@@ -270,9 +269,17 @@
 
     send_texts(0, parts - second * (parts - early))
 
+    loads[0].wait()
+
     @pl.loop(0, 2 * parts)
     def _(i):
         image_copy(i).start()
+
+    for load in loads[1:]:
+        load.wait()
+
+    scale = jnp.exp(jnp.full((1, 1), scale_ref[0], jnp.float32))
+    offset = jnp.full((1, 1), offset_ref[0], jnp.float32)
 
     prepare()
 
@@ -350,7 +357,7 @@
         c = first * s + last * (s - 3 * tiles) + between * ((s + 1) // 2 - 2)
         which = place_row(p)
 
-        @pl.when(s == steps - 1)
+        @pl.when((1 - role) * (s + 1) == steps)
         def _():
             @pl.loop(0, tiles)
             def _(k):
@@ -403,9 +410,17 @@
         def _():
             relay(INNER, 3, 2, 3, 4, c)
 
-        whole = image_part[cut(c), :] + jnp.dot(
-            slopes[OTHER, cut(c), last_tile], unit_texts[last_tile, :], preferred_element_type=jnp.float32)
-        image_sent[cut(c), :] = whole.astype(jnp.bfloat16)
+        @pl.when(is_end)
+        def _():
+            whole = image_part[cut(c), :] + jnp.dot(
+                slopes[OTHER, cut(c), last_tile], unit_texts[last_tile, :], preferred_element_type=jnp.float32)
+            image_sent[cut(c), :] = whole.astype(jnp.bfloat16)
+
+        @pl.when(is_mid)
+        def _():
+            whole = jnp.dot(slopes[OTHER, cut(c), :], unit_texts[...], preferred_element_type=jnp.float32)
+            image_sent[cut(c), :] = whole.astype(jnp.bfloat16)
+
         back_copy(c).start()
         image_acc[cut(c), :] = jnp.dot(
             slopes[OWN, cut(c), :], unit_texts[...], preferred_element_type=jnp.float32)
@@ -540,7 +555,7 @@
             pltpu.VMEM((1, row_count // tiles), jnp.float32),
             pltpu.VMEM((places, 8, 128), jnp.float32),
             pltpu.VMEM((2 * groups, 8, 128), jnp.float32),
-            pltpu.SemaphoreType.DMA((6,)),
+            pltpu.SemaphoreType.DMA((5 + parts,)),
             pltpu.SemaphoreType.DMA((3, 4)),
             pltpu.SemaphoreType.DMA((places, parts)),
             pltpu.SemaphoreType.DMA((2 * parts,)),

time: 90.9 us -> 90.9 us (level)
  no operation moved by 1% of the time
where the time goes in v5:
time: 90.9 us; the launch traced here: 90.8 us
  Pallas kernels  87.1 us (96%)
  between operations  3.7 us (4%)
    pallas_call x1, Pallas kernels, body(): pl.pallas_call(functools.partial(grid_kernel, reach, parts, tiles), out_s...  85.8 us

profile of v5, /device:TPU:0, one launch (start us, length us, event | category | flops | bytes accessed | tf_op | source)
XLA Modules:
  0.0 90.8 jit_solution(2972115577003617171)
XLA Ops:
  1.9 85.8 %shard_map.85 = (bf16[384,1152]{1,0:T(8,128)(2,1)S(1)}, bf16[384,1152]{1,0:T(8,128)(2,1)S(1)}, f32[1]{0:T(128)}) custom-call(s32[8,7]{1,0:T(8,128)} %mask_hbm.1, f32[1]{0:T(128)S(6)} %copy.10.scale_hbm, f32[1]{0:T(128)S(6)} %copy.11.offset_hbm, bf16[384,1152]{1,0:T(8,128)(2,1)} %image_hbm.1, bf16[384,1152]{1,0:T(8,128)(2,1)} %text_hbm.1, s32[1,384]{1,0:T(1,128)} %pos_hbm.1), custom_call_target="tpu_custom_call" | custom-call | tf_op jit(solution)/shard_map/pallas_call | solution.py:527
  87.7 1.3 %shard_map.86 = (bf16[384,1152]{1,0:T(8,128)(2,1)}, bf16[384,1152]{1,0:T(8,128)(2,1)}) custom-call(bf16[384,1152]{1,0:T(8,128)(2,1)S(1)} %get-tuple-element.8.image_ref, bf16[384,1152]{1,0:T(8,128)(2,1)S(1)} %get-tuple-element.9.text_ref), custom_call_target="tpu_custom_call" | custom-call | tf_op jit(solution)/shard_map/pallas_call | solution.py:574
